TPU v7x, 32 devices: a whole 2x2x4 slice. The times are simulated.
32 devices in a mesh: comm: 4 (over z), arc: 8 (over y, x, core).
Axes of the slice: x: 2, y: 2, z: 4, core: 2. Of those that a mesh axis runs over, the one named last changes fastest.
Arguments:
- prev_dist: float32 [512, 2048], P('comm', 'arc'), may hold values from 0 to 4
- source_node: int32 [512], P('comm'), may hold values from 0 to 2047, as said below
- arc_tail: int32 [16, 2048], P(None, 'arc'), may hold values from 0 to 2047, as said below
- base_cost: float32 [16, 2048], P(None, 'arc'), may hold values from 0.05 to 1
- arc_price: float32 [16, 2048], P(None, 'arc'), may hold values from 0 to 1
- capacity: float32 [16, 2048], P(None, 'arc')
- path_arcs: int32 [512, 128], P(('comm', 'arc')), may hold values from 0 to 32767, as said below
- demand: float32 [512], P(('comm', 'arc')), may hold values from 0.5 to 2
Outputs:
- final_dist: float32 [512, 2048], P('comm', 'arc')
- new_price: float32 [16, 2048], P(None, 'arc')
Inputs may be any that keep to these rules, and one draw needn't show every extreme that they name: `arc_tail`: the tail of arc s * 2048 + v lies in a node block (nodes 128 b to 128 b + 127) at most 2 blocks before or after v's block, counted around the cycle of blocks. Row k is a walk: the head of path_arcs[k, h + 1] (its id modulo 2048) is the tail of path_arcs[k, h]. `source_node`: the tail of path_arcs[k, 127].
All inputs are finite; a program needn't handle non-finite values.
Results may differ from a plain program's by a relative error of at most 0.00002.
Values sent between devices are 32-bit elements; how exact they have to be, the bound alone decides.
No kernel may reach another device: no remote copies, remote signals or barrier semaphores. Data moves between devices by JAX's collectives and lax.ppermute only.
A program may use at most 64 MiB of HBM per device.

v0:
```python
import jax
import jax.numpy as jnp
from jax import lax
from jax.sharding import PartitionSpec as P

SWEEPS = 8
step_size = 0.25
eps_value = 1e-06


def with_halo(cells, sides, width):
    for axis, dim in sides:
        count = lax.axis_size(axis)
        head = lax.slice_in_dim(cells, 0, width, axis=dim)
        tail = lax.slice_in_dim(cells, cells.shape[dim] - width, cells.shape[dim], axis=dim)
        cells = jnp.concatenate(
            [
                lax.ppermute(tail, axis, [(i, (i + 1) % count) for i in range(count)]),
                cells,
                lax.ppermute(head, axis, [((i + 1) % count, i) for i in range(count)]),
            ],
            axis=dim,
        )
    return cells


def relax(window, window_start, tail_nodes, weights, current, node_count):
    degree = tail_nodes.shape[0]
    node_span = tail_nodes.shape[1]
    local_index = jnp.mod(tail_nodes - window_start, node_count).reshape(-1)
    picked = jnp.take(window, local_index, axis=0).reshape(degree, node_span, window.shape[1])
    candidate = picked + weights[:, :, None]
    return jnp.minimum(current, jnp.min(candidate, axis=0))


def shards(prev_dist, source_node, arc_tail, base_cost, arc_price, capacity, path_arcs, demand):
    shard_nodes = prev_dist.shape[1]
    arc_devices = lax.axis_size("arc")
    node_count = shard_nodes * arc_devices
    degree = arc_tail.shape[0]
    sweep_total = SWEEPS
    first_node = lax.axis_index("arc") * shard_nodes
    node_ids = first_node + jnp.arange(shard_nodes, dtype=jnp.int32)
    arc_weight = base_cost + arc_price
    node_major = jnp.where(node_ids[:, None] == source_node[None, :], jnp.float32(0.0), prev_dist.T)
    for sweep_number in range(sweep_total):
        window = with_halo(node_major, (("arc", 0),), shard_nodes)
        node_major = relax(
            window, first_node - shard_nodes, arc_tail, arc_weight, node_major, node_count
        )
    distance = node_major.T
    amounts = jnp.broadcast_to(demand[:, None], path_arcs.shape).reshape(-1)
    flattened = (
        jnp.zeros((degree * node_count,), jnp.float32).at[path_arcs.reshape(-1)].add(amounts)
    )
    partial_flow = lax.psum_scatter(
        flattened.reshape(degree, node_count), "arc", scatter_dimension=1, tiled=True
    )
    arc_flow = lax.psum(partial_flow, "comm")
    gradient = arc_flow - capacity
    square_sum = lax.psum(jnp.sum(gradient * gradient), "arc")
    scale_root = jnp.sqrt(square_sum / (degree * node_count) + eps_value)
    new_price = jnp.maximum(arc_price + step_size * gradient / scale_root, jnp.float32(0.0))
    return (distance, new_price)


def solution(mesh):
    in_specs = (
        P("comm", "arc"),
        P("comm"),
        P(None, "arc"),
        P(None, "arc"),
        P(None, "arc"),
        P(None, "arc"),
        P(("comm", "arc"), None),
        P(("comm", "arc")),
    )
    out_specs = (P("comm", "arc"), P(None, "arc"))
    return jax.shard_map(shards, mesh=mesh, in_specs=in_specs, out_specs=out_specs, check_vma=False)
```

profile of v0, /device:TPU:0, one launch (start us, length us, event | category | flops | bytes accessed | tf_op | source)
XLA Modules:
  0.0 245.0 jit_solution(11023003977533881316)
XLA Ops:
  9.0 3.4 %collective-permute-start.1 = (f32[256,128]{1,0:T(8,128)S(1)}, f32[256,128]{1,0:T(8,128)S(1)}, u32[]{:S(2)}, u32[]{:S(2)}) collective-permute-start(f32[256,128]{1,0:T(8,128)S(1)} %bitcast_select_fusion), channel_id=1, source_target_pairs={{1,0},{2,1},{3,2},{4,3},{5,4},{6,5},{7,6},{0,7},{9,8},{10,9},{11,1... | collective-permute-start | bytes 393224 | tf_op jit(solution)/shard_map/ppermute | solution.py:20
  13.2 11.3 %scatter_custom_fusion = f32[32768]{0:T(1024)S(1)} fusion(s32[2048]{0:T(1024)S(1)} %bitcast.60, f32[2048]{0:T(1024)S(1)} %broadcast_bitcast_fusion, f32[]{:T(128)} %constant.60.clone.1), kind=kCustom, calls=%fused_computation.42 | custom fusion | flops 2048 | bytes 131076 | tf_op jit(solution)/shard_map/scatter-add | solution.py:54
  26.1 14.1 %gather_fusion = f32[4096,128]{1,0:T(8,128)} fusion(f32[768,128]{1,0:T(8,128)S(1)} %pad_maximum_fusion, s32[4096]{0:T(1024)S(1)} %fusion.4), kind=kCustom, calls=%fused_computation.clone | custom fusion | bytes 4210688 | tf_op jit(solution)/shard_map/jit(_take)/gather | solution.py:31
  40.2 20.2 %reduce-scatter.2.cloned.1.call-done = f32[16,256]{1,0:T(8,128)} async-done(((f32[16,2048]{1,0:T(8,128)}), f32[16,256]{1,0:T(8,128)}) %reduce-scatter.2.cloned.1.call-update) | async-done | bytes 16400 | tf_op jit(solution)/shard_map/reduce_scatter | solution.py:56
  60.4 19.4 %psum.14 = f32[16,256]{1,0:T(8,128)S(1)} all-reduce(f32[16,256]{1,0:T(8,128)} %reduce-scatter.2.cloned.1.call-done), channel_id=1, replica_groups=mesh['comm'=4,'arc'=8] {'comm'}, use_global_device_ids=true, to_apply=%region_10.12 | all-reduce | flops 4096 | bytes 32768 | tf_op jit(solution)/shard_map/psum | solution.py:59
  80.4 3.6 %broadcast_select_fusion.7 = f32[4096,128]{1,0:T(8,128)S(1)} fusion(f32[4096,128]{1,0:T(8,128)} %gather_fusion, pred[4096]{0:T(1024)(128)(4,1)S(1)} %compare_and_fusion), kind=kLoop, calls=%fused_computation.24 | loop fusion | flops 524288 | bytes 4198400 | tf_op jit(solution)/shard_map/jit(_take)/select_n | solution.py:31
  84.0 12.5 %psum.15 = f32[]{:T(128)} all-reduce(f32[]{:T(128)} %multiply_reduce_fusion), channel_id=1, replica_groups=mesh['comm'=4,'arc'=8] {'arc'}, use_global_device_ids=true, to_apply=%region_12.14 | all-reduce | flops 1 | bytes 8 | tf_op jit(solution)/shard_map/psum | solution.py:61
  99.2 2.5 %collective-permute-done.3 = f32[256,128]{1,0:T(8,128)S(1)} collective-permute-done((f32[256,128]{1,0:T(8,128)S(1)}, f32[256,128]{1,0:T(8,128)S(1)}, u32[]{:S(2)}, u32[]{:S(2)}) %collective-permute-start.3) | collective-permute-done | bytes 131104 | tf_op jit(solution)/shard_map/ppermute | solution.py:20
  101.7 3.7 %collective-permute-done.2 = f32[256,128]{1,0:T(8,128)S(1)} collective-permute-done((f32[256,128]{1,0:T(8,128)S(1)}, f32[256,128]{1,0:T(8,128)S(1)}, u32[]{:S(2)}, u32[]{:S(2)}) %collective-permute-start.2) | collective-permute-done | bytes 131104 | tf_op jit(solution)/shard_map/ppermute | solution.py:18
  105.4 10.8 %gather_fusion.1 = f32[4096,128]{1,0:T(8,128)S(1)} fusion(f32[768,128]{1,0:T(8,128)S(1)} %pad_maximum_fusion.1, s32[4096]{0:T(1024)S(1)} %fusion.4), kind=kCustom, calls=%fused_computation.1.clone | custom fusion | bytes 4210688 | tf_op jit(solution)/shard_map/jit(_take)/gather | solution.py:31
  119.7 3.2 %collective-permute-done.5 = f32[256,128]{1,0:T(8,128)S(1)} collective-permute-done((f32[256,128]{1,0:T(8,128)S(1)}, f32[256,128]{1,0:T(8,128)S(1)}, u32[]{:S(2)}, u32[]{:S(2)}) %collective-permute-start.5) | collective-permute-done | bytes 131104 | tf_op jit(solution)/shard_map/ppermute | solution.py:20
  122.9 2.3 collective-permute-done.4
  125.2 10.8 %gather_fusion.2 = f32[4096,128]{1,0:T(8,128)S(1)} fusion(f32[768,128]{1,0:T(8,128)S(1)} %pad_maximum_fusion.2, s32[4096]{0:T(1024)S(1)} %fusion.4), kind=kCustom, calls=%fused_computation.2.clone | custom fusion | bytes 4210688 | tf_op jit(solution)/shard_map/jit(_take)/gather | solution.py:31
  139.5 3.2 %collective-permute-done.7 = f32[256,128]{1,0:T(8,128)S(1)} collective-permute-done((f32[256,128]{1,0:T(8,128)S(1)}, f32[256,128]{1,0:T(8,128)S(1)}, u32[]{:S(2)}, u32[]{:S(2)}) %collective-permute-start.7) | collective-permute-done | bytes 131104 | tf_op jit(solution)/shard_map/ppermute | solution.py:20
  144.7 10.8 %gather_fusion.3 = f32[4096,128]{1,0:T(8,128)S(1)} fusion(f32[768,128]{1,0:T(8,128)S(1)} %pad_maximum_fusion.3, s32[4096]{0:T(1024)S(1)} %fusion.4), kind=kCustom, calls=%fused_computation.3.clone | custom fusion | bytes 4210688 | tf_op jit(solution)/shard_map/jit(_take)/gather | solution.py:31
  159.2 2.9 %collective-permute-done.9 = f32[256,128]{1,0:T(8,128)S(1)} collective-permute-done((f32[256,128]{1,0:T(8,128)S(1)}, f32[256,128]{1,0:T(8,128)S(1)}, u32[]{:S(2)}, u32[]{:S(2)}) %collective-permute-start.9) | collective-permute-done | bytes 131104 | tf_op jit(solution)/shard_map/ppermute | solution.py:20
  164.6 10.8 %gather_fusion.4 = f32[4096,128]{1,0:T(8,128)S(1)} fusion(f32[768,128]{1,0:T(8,128)S(1)} %pad_maximum_fusion.4, s32[4096]{0:T(1024)S(1)} %fusion.4), kind=kCustom, calls=%fused_computation.4.clone | custom fusion | bytes 4210688 | tf_op jit(solution)/shard_map/jit(_take)/gather | solution.py:31
  178.8 3.2 %collective-permute-done.11 = f32[256,128]{1,0:T(8,128)S(1)} collective-permute-done((f32[256,128]{1,0:T(8,128)S(1)}, f32[256,128]{1,0:T(8,128)S(1)}, u32[]{:S(2)}, u32[]{:S(2)}) %collective-permute-start.11) | collective-permute-done | bytes 131104 | tf_op jit(solution)/shard_map/ppermute | solution.py:20
  184.1 10.8 %gather_fusion.5 = f32[4096,128]{1,0:T(8,128)S(1)} fusion(f32[768,128]{1,0:T(8,128)S(1)} %pad_maximum_fusion.5, s32[4096]{0:T(1024)S(1)} %fusion.4), kind=kCustom, calls=%fused_computation.5.clone | custom fusion | bytes 4210688 | tf_op jit(solution)/shard_map/jit(_take)/gather | solution.py:31
  198.5 2.9 %collective-permute-done.13 = f32[256,128]{1,0:T(8,128)S(1)} collective-permute-done((f32[256,128]{1,0:T(8,128)S(1)}, f32[256,128]{1,0:T(8,128)S(1)}, u32[]{:S(2)}, u32[]{:S(2)}) %collective-permute-start.13) | collective-permute-done | bytes 131104 | tf_op jit(solution)/shard_map/ppermute | solution.py:20
  201.5 2.3 collective-permute-done.12
  203.9 10.8 %gather_fusion.6 = f32[4096,128]{1,0:T(8,128)S(1)} fusion(f32[768,128]{1,0:T(8,128)S(1)} %pad_maximum_fusion.6, s32[4096]{0:T(1024)S(1)} %fusion.4), kind=kCustom, calls=%fused_computation.6.clone | custom fusion | bytes 4210688 | tf_op jit(solution)/shard_map/jit(_take)/gather | solution.py:31
  218.1 3.2 %collective-permute-done.15 = f32[256,128]{1,0:T(8,128)S(1)} collective-permute-done((f32[256,128]{1,0:T(8,128)S(1)}, f32[256,128]{1,0:T(8,128)S(1)}, u32[]{:S(2)}, u32[]{:S(2)}) %collective-permute-start.15) | collective-permute-done | bytes 131104 | tf_op jit(solution)/shard_map/ppermute | solution.py:20
  223.4 10.8 %gather_fusion.7 = f32[4096,128]{1,0:T(8,128)S(1)} fusion(f32[768,128]{1,0:T(8,128)S(1)} %pad_maximum_fusion.7, s32[4096]{0:T(1024)S(1)} %fusion.4), kind=kCustom, calls=%fused_computation.7.clone | custom fusion | bytes 4210688 | tf_op jit(solution)/shard_map/jit(_take)/gather | solution.py:31
  (85 shorter events, 40.3 us)
Async XLA Ops:
  7.2 6.0 %copy-start = (f32[16]{0:T(128)S(1)}, f32[16]{0:T(128)}, u32[]{:S(2)}) copy-start(f32[16]{0:T(128)} %param.17) | copy-start | bytes 196
  7.2 53.2 %reduce-scatter.2.cloned.1.call-start = ((), (), s32[]{:S(2)}) async-start(), calls=%async_computation.1 | async-start | bytes 147456 | tf_op jit(solution)/shard_map/reduce_scatter | solution.py:56
  9.0 17.0 %collective-permute-start.1 = (f32[256,128]{1,0:T(8,128)S(1)}, f32[256,128]{1,0:T(8,128)S(1)}, u32[]{:S(2)}, u32[]{:S(2)}) collective-permute-start(f32[256,128]{1,0:T(8,128)S(1)} %bitcast_select_fusion), channel_id=1, source_target_pairs={{1,0},{2,1},{3,2},{4,3},{5,4},{6,5},{7,6},{0,7},{9,8},{10,9},{11,1... | collective-permute-start | bytes 393224 | tf_op jit(solution)/shard_map/ppermute | solution.py:20
  12.4 13.6 %collective-permute-start = (f32[256,128]{1,0:T(8,128)S(1)}, f32[256,128]{1,0:T(8,128)S(1)}, u32[]{:S(2)}, u32[]{:S(2)}) collective-permute-start(f32[256,128]{1,0:T(8,128)S(1)} %bitcast_select_fusion), channel_id=1, source_target_pairs={{0,1},{1,2},{2,3},{3,4},{4,5},{5,6},{6,7},{7,0},{8,9},{9,10},{10,1... | collective-permute-start | bytes 393224 | tf_op jit(solution)/shard_map/ppermute | solution.py:18
  26.1 53.7 %copy-start.5 = (f32[16,256]{1,0:T(8,128)S(1)}, f32[16,256]{1,0:T(8,128)}, u32[]{:S(2)}) copy-start(f32[16,256]{1,0:T(8,128)} %param.15) | copy-start | bytes 49156
  80.4 16.8 %copy-start.6 = (f32[16,256]{1,0:T(8,128)S(1)}, f32[16,256]{1,0:T(8,128)}, u32[]{:S(2)}) copy-start(f32[16,256]{1,0:T(8,128)} %param.14) | copy-start | bytes 49156
  80.4 16.8 %copy-start.7 = (f32[16,256]{1,0:T(8,128)S(1)}, f32[16,256]{1,0:T(8,128)}, u32[]{:S(2)}) copy-start(f32[16,256]{1,0:T(8,128)} %param.13) | copy-start | bytes 49156
  84.0 14.5 %copy-start.8 = (s32[128]{0:T(128)S(1)}, s32[128]{0:T(128)}, u32[]{:S(2)}) copy-start(s32[128]{0:T(128)} %param.11) | copy-start | bytes 1540
  98.5 17.7 %copy-start.3 = (f32[256,128]{1,0:T(8,128)}, f32[256,128]{1,0:T(8,128)S(1)}, u32[]{:S(2)}) copy-start(f32[256,128]{1,0:T(8,128)S(1)} %add_reduce_fusion.7) | copy-start | bytes 393220
  98.6 3.0 %collective-permute-start.3 = (f32[256,128]{1,0:T(8,128)S(1)}, f32[256,128]{1,0:T(8,128)S(1)}, u32[]{:S(2)}, u32[]{:S(2)}) collective-permute-start(f32[256,128]{1,0:T(8,128)S(1)} %fusion.5), channel_id=1, source_target_pairs={{1,0},{2,1},{3,2},{4,3},{5,4},{6,5},{7,6},{0,7},{9,8},{10,9},{11,1... | collective-permute-start | bytes 393224 | tf_op jit(solution)/shard_map/ppermute | solution.py:20
  98.7 6.7 %collective-permute-start.2 = (f32[256,128]{1,0:T(8,128)S(1)}, f32[256,128]{1,0:T(8,128)S(1)}, u32[]{:S(2)}, u32[]{:S(2)}) collective-permute-start(f32[256,128]{1,0:T(8,128)S(1)} %fusion.5), channel_id=1, source_target_pairs={{0,1},{1,2},{2,3},{3,4},{4,5},{5,6},{6,7},{7,0},{8,9},{9,10},{10,1... | collective-permute-start | bytes 393224 | tf_op jit(solution)/shard_map/ppermute | solution.py:18
  119.1 3.8 %collective-permute-start.5 = (f32[256,128]{1,0:T(8,128)S(1)}, f32[256,128]{1,0:T(8,128)S(1)}, u32[]{:S(2)}, u32[]{:S(2)}) collective-permute-start(f32[256,128]{1,0:T(8,128)S(1)} %min.49), channel_id=1, source_target_pairs={{1,0},{2,1},{3,2},{4,3},{5,4},{6,5},{7,6},{0,7},{9,8},{10,9},{11,1... | collective-permute-start | bytes 393224 | tf_op jit(solution)/shard_map/ppermute | solution.py:20
  119.2 6.0 %collective-permute-start.4 = (f32[256,128]{1,0:T(8,128)S(1)}, f32[256,128]{1,0:T(8,128)S(1)}, u32[]{:S(2)}, u32[]{:S(2)}) collective-permute-start(f32[256,128]{1,0:T(8,128)S(1)} %min.49), channel_id=1, source_target_pairs={{0,1},{1,2},{2,3},{3,4},{4,5},{5,6},{6,7},{7,0},{8,9},{9,10},{10,1... | collective-permute-start | bytes 393224 | tf_op jit(solution)/shard_map/ppermute | solution.py:18
  138.9 3.8 %collective-permute-start.7 = (f32[256,128]{1,0:T(8,128)S(1)}, f32[256,128]{1,0:T(8,128)S(1)}, u32[]{:S(2)}, u32[]{:S(2)}) collective-permute-start(f32[256,128]{1,0:T(8,128)S(1)} %min.51), channel_id=1, source_target_pairs={{1,0},{2,1},{3,2},{4,3},{5,4},{6,5},{7,6},{0,7},{9,8},{10,9},{11,1... | collective-permute-start | bytes 393224 | tf_op jit(solution)/shard_map/ppermute | solution.py:20
  139.4 5.3 %collective-permute-start.6 = (f32[256,128]{1,0:T(8,128)S(1)}, f32[256,128]{1,0:T(8,128)S(1)}, u32[]{:S(2)}, u32[]{:S(2)}) collective-permute-start(f32[256,128]{1,0:T(8,128)S(1)} %min.51), channel_id=1, source_target_pairs={{0,1},{1,2},{2,3},{3,4},{4,5},{5,6},{6,7},{7,0},{8,9},{9,10},{10,1... | collective-permute-start | bytes 393224 | tf_op jit(solution)/shard_map/ppermute | solution.py:18
  158.4 3.8 %collective-permute-start.9 = (f32[256,128]{1,0:T(8,128)S(1)}, f32[256,128]{1,0:T(8,128)S(1)}, u32[]{:S(2)}, u32[]{:S(2)}) collective-permute-start(f32[256,128]{1,0:T(8,128)S(1)} %min.53), channel_id=1, source_target_pairs={{1,0},{2,1},{3,2},{4,3},{5,4},{6,5},{7,6},{0,7},{9,8},{10,9},{11,1... | collective-permute-start | bytes 393224 | tf_op jit(solution)/shard_map/ppermute | solution.py:20
  159.2 5.3 %collective-permute-start.8 = (f32[256,128]{1,0:T(8,128)S(1)}, f32[256,128]{1,0:T(8,128)S(1)}, u32[]{:S(2)}, u32[]{:S(2)}) collective-permute-start(f32[256,128]{1,0:T(8,128)S(1)} %min.53), channel_id=1, source_target_pairs={{0,1},{1,2},{2,3},{3,4},{4,5},{5,6},{6,7},{7,0},{8,9},{9,10},{10,1... | collective-permute-start | bytes 393224 | tf_op jit(solution)/shard_map/ppermute | solution.py:18
  178.2 3.8 %collective-permute-start.11 = (f32[256,128]{1,0:T(8,128)S(1)}, f32[256,128]{1,0:T(8,128)S(1)}, u32[]{:S(2)}, u32[]{:S(2)}) collective-permute-start(f32[256,128]{1,0:T(8,128)S(1)} %min.55), channel_id=1, source_target_pairs={{1,0},{2,1},{3,2},{4,3},{5,4},{6,5},{7,6},{0,7},{9,8},{10,9},{11,1... | collective-permute-start | bytes 393224 | tf_op jit(solution)/shard_map/ppermute | solution.py:20
  178.7 5.3 %collective-permute-start.10 = (f32[256,128]{1,0:T(8,128)S(1)}, f32[256,128]{1,0:T(8,128)S(1)}, u32[]{:S(2)}, u32[]{:S(2)}) collective-permute-start(f32[256,128]{1,0:T(8,128)S(1)} %min.55), channel_id=1, source_target_pairs={{0,1},{1,2},{2,3},{3,4},{4,5},{5,6},{6,7},{7,0},{8,9},{9,10},{10,1... | collective-permute-start | bytes 393224 | tf_op jit(solution)/shard_map/ppermute | solution.py:18
  197.7 6.2 %copy-start.1 = (f32[256,128]{1,0:T(8,128)}, f32[256,128]{1,0:T(8,128)S(1)}, u32[]{:S(2)}) copy-start(f32[256,128]{1,0:T(8,128)S(1)} %add_reduce_fusion.2) | copy-start | bytes 393220
  197.7 3.8 %collective-permute-start.13 = (f32[256,128]{1,0:T(8,128)S(1)}, f32[256,128]{1,0:T(8,128)S(1)}, u32[]{:S(2)}, u32[]{:S(2)}) collective-permute-start(f32[256,128]{1,0:T(8,128)S(1)} %min.57), channel_id=1, source_target_pairs={{1,0},{2,1},{3,2},{4,3},{5,4},{6,5},{7,6},{0,7},{9,8},{10,9},{11,1... | collective-permute-start | bytes 393224 | tf_op jit(solution)/shard_map/ppermute | solution.py:20
  198.5 5.3 %collective-permute-start.12 = (f32[256,128]{1,0:T(8,128)S(1)}, f32[256,128]{1,0:T(8,128)S(1)}, u32[]{:S(2)}, u32[]{:S(2)}) collective-permute-start(f32[256,128]{1,0:T(8,128)S(1)} %min.57), channel_id=1, source_target_pairs={{0,1},{1,2},{2,3},{3,4},{4,5},{5,6},{6,7},{7,0},{8,9},{9,10},{10,1... | collective-permute-start | bytes 393224 | tf_op jit(solution)/shard_map/ppermute | solution.py:18
  217.5 3.8 %collective-permute-start.15 = (f32[256,128]{1,0:T(8,128)S(1)}, f32[256,128]{1,0:T(8,128)S(1)}, u32[]{:S(2)}, u32[]{:S(2)}) collective-permute-start(f32[256,128]{1,0:T(8,128)S(1)} %min.59), channel_id=1, source_target_pairs={{1,0},{2,1},{3,2},{4,3},{5,4},{6,5},{7,6},{0,7},{9,8},{10,9},{11,1... | collective-permute-start | bytes 393224 | tf_op jit(solution)/shard_map/ppermute | solution.py:20
  218.0 5.3 %collective-permute-start.14 = (f32[256,128]{1,0:T(8,128)S(1)}, f32[256,128]{1,0:T(8,128)S(1)}, u32[]{:S(2)}, u32[]{:S(2)}) collective-permute-start(f32[256,128]{1,0:T(8,128)S(1)} %min.59), channel_id=1, source_target_pairs={{0,1},{1,2},{2,3},{3,4},{4,5},{5,6},{6,7},{7,0},{8,9},{9,10},{10,1... | collective-permute-start | bytes 393224 | tf_op jit(solution)/shard_map/ppermute | solution.py:18
  (2 other events, 1.9 us)
Sparse Core Ops, SparseCore 0:
  25.3 35.0 reduce-scatter.1
where the time goes:
time: 245 us
  local copies, waits for them, and re-layouts  92.3 us (38%)
  waiting for transfers between devices  58.3 us (24%)
  other arithmetic  39.5 us (16%)
  blocking collectives  31.8 us (13%)
  between operations  15.2 us (6%)
  starting transfers between devices  7.89 us (3%)
    gather x8, local copies, waits for them, and re-layouts, relax(): jnp.take(window, local_index, axis=0)  89.5 us
    ppermute x8, waiting for transfers between devices, with_halo(): lax.ppermute(head, axis, [((i + 1) % count, i) for i in range(count)])  21.2 us
    reduce_scatter x1, waiting for transfers between devices, shards(): lax.psum_scatter(flattened.reshape(degree, node_count), 'arc', scatter_di...  20.2 us
    psum x1, blocking collectives, shards(): arc_flow = lax.psum(partial_flow, 'comm')  19.4 us
    select_n x8, other arithmetic, relax(): jnp.take(window, local_index, axis=0)  18.6 us
    ppermute x8, waiting for transfers between devices, with_halo(): lax.ppermute(tail, axis, [(i, (i + 1) % count) for i in range(count)])  16.9 us
    psum x1, blocking collectives, shards(): square_sum = lax.psum(jnp.sum(gradient * gradient), 'arc')  12.5 us
    scatter-add x1, other arithmetic, shards(): jnp.zeros((degree * node_count,), jnp.float32).at[path_arcs.reshape(-1)]  11.3 us
  transfers between devices with their start and end apart: 17, of which 15 were waited for; matrix products, arithmetic and copies ran while one was open for 11% of the time, Pallas kernels for 0%

commit v1 on v0

--- a/solution.py
+++ b/solution.py
@@ -56,7 +56,7 @@
     partial_flow = lax.psum_scatter(
         flattened.reshape(degree, node_count), "arc", scatter_dimension=1, tiled=True
     )
-    arc_flow = lax.psum(partial_flow, "comm")
+    arc_flow = jnp.sum(lax.all_gather(partial_flow, "comm"), axis=0)
     gradient = arc_flow - capacity
     square_sum = lax.psum(jnp.sum(gradient * gradient), "arc")
     scale_root = jnp.sqrt(square_sum / (degree * node_count) + eps_value)

time: 245 us -> 239 us (0.976)
  blocking collectives: 31.8 us -> 25.9 us
    psum x1 -> x0, blocking collectives: 19.4 us -> none  [shards(): arc_flow = lax.psum(partial_flow, 'comm')]
    all_gather x0 -> x1, blocking collectives: none -> 13.5 us  [shards(): arc_flow = jnp.sum(lax.all_gather(partial_flow, 'comm'), axis=0)]
  transfers between devices with their start and end apart: 17 -> 17, of which waited for: 15 -> 15; matrix products, arithmetic and copies ran while one was open for 11% -> 12% of each run, Pallas kernels for 0% -> 0%
where the time goes in v1:
time: 239 us
  local copies, waits for them, and re-layouts  92.3 us (39%)
  waiting for transfers between devices  58.3 us (24%)
  other arithmetic  39.5 us (17%)
  blocking collectives  25.9 us (11%)
  between operations  15.2 us (6%)
  starting transfers between devices  7.89 us (3%)
    gather x8, local copies, waits for them, and re-layouts, relax(): jnp.take(window, local_index, axis=0)  89.5 us
    ppermute x8, waiting for transfers between devices, with_halo(): lax.ppermute(head, axis, [((i + 1) % count, i) for i in range(count)])  21.2 us
    reduce_scatter x1, waiting for transfers between devices, shards(): lax.psum_scatter(flattened.reshape(degree, node_count), 'arc', scatter_di...  20.2 us
    select_n x8, other arithmetic, relax(): jnp.take(window, local_index, axis=0)  18.6 us
    ppermute x8, waiting for transfers between devices, with_halo(): lax.ppermute(tail, axis, [(i, (i + 1) % count) for i in range(count)])  16.9 us
    all_gather x1, blocking collectives, shards(): arc_flow = jnp.sum(lax.all_gather(partial_flow, 'comm'), axis=0)  13.5 us
    psum x1, blocking collectives, shards(): square_sum = lax.psum(jnp.sum(gradient * gradient), 'arc')  12.5 us
    scatter-add x1, other arithmetic, shards(): jnp.zeros((degree * node_count,), jnp.float32).at[path_arcs.reshape(-1)]  11.3 us
  transfers between devices with their start and end apart: 17, of which 15 were waited for; matrix products, arithmetic and copies ran while one was open for 12% of the time, Pallas kernels for 0%

profile of v1, /device:TPU:0, one launch (start us, length us, event | category | flops | bytes accessed | tf_op | source)
XLA Modules:
  0.0 239.1 jit_solution(13242958989153119184)
XLA Ops:
  9.0 3.4 %collective-permute-start.1 = (f32[256,128]{1,0:T(8,128)S(1)}, f32[256,128]{1,0:T(8,128)S(1)}, u32[]{:S(2)}, u32[]{:S(2)}) collective-permute-start(f32[256,128]{1,0:T(8,128)S(1)} %bitcast_select_fusion), channel_id=1, source_target_pairs={{1,0},{2,1},{3,2},{4,3},{5,4},{6,5},{7,6},{0,7},{9,8},{10,9},{11,1... | collective-permute-start | bytes 393224 | tf_op jit(solution)/shard_map/ppermute | solution.py:20
  13.2 11.3 %scatter_custom_fusion = f32[32768]{0:T(1024)S(1)} fusion(s32[2048]{0:T(1024)S(1)} %bitcast.62, f32[2048]{0:T(1024)S(1)} %broadcast_bitcast_fusion, f32[]{:T(128)} %constant.60.clone.1), kind=kCustom, calls=%fused_computation.42 | custom fusion | flops 2048 | bytes 131076 | tf_op jit(solution)/shard_map/scatter-add | solution.py:54
  26.1 14.1 %gather_fusion = f32[4096,128]{1,0:T(8,128)} fusion(f32[768,128]{1,0:T(8,128)S(1)} %pad_maximum_fusion, s32[4096]{0:T(1024)S(1)} %fusion.4), kind=kCustom, calls=%fused_computation.clone | custom fusion | bytes 4210688 | tf_op jit(solution)/shard_map/jit(_take)/gather | solution.py:31
  40.2 20.2 %reduce-scatter.2.cloned.1.call-done = f32[16,256]{1,0:T(8,128)} async-done(((f32[16,2048]{1,0:T(8,128)}), f32[16,256]{1,0:T(8,128)}) %reduce-scatter.2.cloned.1.call-update) | async-done | bytes 16400 | tf_op jit(solution)/shard_map/reduce_scatter | solution.py:56
  60.4 13.5 %all-gather = f32[64,256]{1,0:T(8,128)S(1)} all-gather(f32[16,256]{1,0:T(8,128)} %reduce-scatter.2.cloned.1.call-done), channel_id=2, replica_groups=mesh['comm'=4,'arc'=8] {'comm'}, dimensions={0}, use_global_device_ids=true | all-gather | bytes 81920 | tf_op jit(solution)/shard_map/all_gather | solution.py:59
  74.5 3.6 %broadcast_select_fusion.7 = f32[4096,128]{1,0:T(8,128)S(1)} fusion(f32[4096,128]{1,0:T(8,128)} %gather_fusion, pred[4096]{0:T(1024)(128)(4,1)S(1)} %compare_and_fusion), kind=kLoop, calls=%fused_computation.24 | loop fusion | flops 524288 | bytes 4198400 | tf_op jit(solution)/shard_map/jit(_take)/select_n | solution.py:31
  78.1 12.5 %psum.7 = f32[]{:T(128)} all-reduce(f32[]{:T(128)} %multiply_reduce_fusion), channel_id=1, replica_groups=mesh['comm'=4,'arc'=8] {'arc'}, use_global_device_ids=true, to_apply=%region_12.14 | all-reduce | flops 1 | bytes 8 | tf_op jit(solution)/shard_map/psum | solution.py:61
  93.3 2.5 %collective-permute-done.3 = f32[256,128]{1,0:T(8,128)S(1)} collective-permute-done((f32[256,128]{1,0:T(8,128)S(1)}, f32[256,128]{1,0:T(8,128)S(1)}, u32[]{:S(2)}, u32[]{:S(2)}) %collective-permute-start.3) | collective-permute-done | bytes 131104 | tf_op jit(solution)/shard_map/ppermute | solution.py:20
  95.8 3.7 %collective-permute-done.2 = f32[256,128]{1,0:T(8,128)S(1)} collective-permute-done((f32[256,128]{1,0:T(8,128)S(1)}, f32[256,128]{1,0:T(8,128)S(1)}, u32[]{:S(2)}, u32[]{:S(2)}) %collective-permute-start.2) | collective-permute-done | bytes 131104 | tf_op jit(solution)/shard_map/ppermute | solution.py:18
  99.6 10.8 %gather_fusion.1 = f32[4096,128]{1,0:T(8,128)S(1)} fusion(f32[768,128]{1,0:T(8,128)S(1)} %pad_maximum_fusion.1, s32[4096]{0:T(1024)S(1)} %fusion.4), kind=kCustom, calls=%fused_computation.1.clone | custom fusion | bytes 4210688 | tf_op jit(solution)/shard_map/jit(_take)/gather | solution.py:31
  113.8 3.2 %collective-permute-done.5 = f32[256,128]{1,0:T(8,128)S(1)} collective-permute-done((f32[256,128]{1,0:T(8,128)S(1)}, f32[256,128]{1,0:T(8,128)S(1)}, u32[]{:S(2)}, u32[]{:S(2)}) %collective-permute-start.5) | collective-permute-done | bytes 131104 | tf_op jit(solution)/shard_map/ppermute | solution.py:20
  117.0 2.3 collective-permute-done.4
  119.4 10.8 %gather_fusion.2 = f32[4096,128]{1,0:T(8,128)S(1)} fusion(f32[768,128]{1,0:T(8,128)S(1)} %pad_maximum_fusion.2, s32[4096]{0:T(1024)S(1)} %fusion.4), kind=kCustom, calls=%fused_computation.2.clone | custom fusion | bytes 4210688 | tf_op jit(solution)/shard_map/jit(_take)/gather | solution.py:31
  133.6 3.2 %collective-permute-done.7 = f32[256,128]{1,0:T(8,128)S(1)} collective-permute-done((f32[256,128]{1,0:T(8,128)S(1)}, f32[256,128]{1,0:T(8,128)S(1)}, u32[]{:S(2)}, u32[]{:S(2)}) %collective-permute-start.7) | collective-permute-done | bytes 131104 | tf_op jit(solution)/shard_map/ppermute | solution.py:20
  138.9 10.8 %gather_fusion.3 = f32[4096,128]{1,0:T(8,128)S(1)} fusion(f32[768,128]{1,0:T(8,128)S(1)} %pad_maximum_fusion.3, s32[4096]{0:T(1024)S(1)} %fusion.4), kind=kCustom, calls=%fused_computation.3.clone | custom fusion | bytes 4210688 | tf_op jit(solution)/shard_map/jit(_take)/gather | solution.py:31
  153.4 2.9 %collective-permute-done.9 = f32[256,128]{1,0:T(8,128)S(1)} collective-permute-done((f32[256,128]{1,0:T(8,128)S(1)}, f32[256,128]{1,0:T(8,128)S(1)}, u32[]{:S(2)}, u32[]{:S(2)}) %collective-permute-start.9) | collective-permute-done | bytes 131104 | tf_op jit(solution)/shard_map/ppermute | solution.py:20
  158.7 10.8 %gather_fusion.4 = f32[4096,128]{1,0:T(8,128)S(1)} fusion(f32[768,128]{1,0:T(8,128)S(1)} %pad_maximum_fusion.4, s32[4096]{0:T(1024)S(1)} %fusion.4), kind=kCustom, calls=%fused_computation.4.clone | custom fusion | bytes 4210688 | tf_op jit(solution)/shard_map/jit(_take)/gather | solution.py:31
  172.9 3.2 %collective-permute-done.11 = f32[256,128]{1,0:T(8,128)S(1)} collective-permute-done((f32[256,128]{1,0:T(8,128)S(1)}, f32[256,128]{1,0:T(8,128)S(1)}, u32[]{:S(2)}, u32[]{:S(2)}) %collective-permute-start.11) | collective-permute-done | bytes 131104 | tf_op jit(solution)/shard_map/ppermute | solution.py:20
  178.2 10.8 %gather_fusion.5 = f32[4096,128]{1,0:T(8,128)S(1)} fusion(f32[768,128]{1,0:T(8,128)S(1)} %pad_maximum_fusion.5, s32[4096]{0:T(1024)S(1)} %fusion.4), kind=kCustom, calls=%fused_computation.5.clone | custom fusion | bytes 4210688 | tf_op jit(solution)/shard_map/jit(_take)/gather | solution.py:31
  192.7 2.9 %collective-permute-done.13 = f32[256,128]{1,0:T(8,128)S(1)} collective-permute-done((f32[256,128]{1,0:T(8,128)S(1)}, f32[256,128]{1,0:T(8,128)S(1)}, u32[]{:S(2)}, u32[]{:S(2)}) %collective-permute-start.13) | collective-permute-done | bytes 131104 | tf_op jit(solution)/shard_map/ppermute | solution.py:20
  195.6 2.3 collective-permute-done.12
  198.0 10.8 %gather_fusion.6 = f32[4096,128]{1,0:T(8,128)S(1)} fusion(f32[768,128]{1,0:T(8,128)S(1)} %pad_maximum_fusion.6, s32[4096]{0:T(1024)S(1)} %fusion.4), kind=kCustom, calls=%fused_computation.6.clone | custom fusion | bytes 4210688 | tf_op jit(solution)/shard_map/jit(_take)/gather | solution.py:31
  212.2 3.2 %collective-permute-done.15 = f32[256,128]{1,0:T(8,128)S(1)} collective-permute-done((f32[256,128]{1,0:T(8,128)S(1)}, f32[256,128]{1,0:T(8,128)S(1)}, u32[]{:S(2)}, u32[]{:S(2)}) %collective-permute-start.15) | collective-permute-done | bytes 131104 | tf_op jit(solution)/shard_map/ppermute | solution.py:20
  217.5 10.8 %gather_fusion.7 = f32[4096,128]{1,0:T(8,128)S(1)} fusion(f32[768,128]{1,0:T(8,128)S(1)} %pad_maximum_fusion.7, s32[4096]{0:T(1024)S(1)} %fusion.4), kind=kCustom, calls=%fused_computation.7.clone | custom fusion | bytes 4210688 | tf_op jit(solution)/shard_map/jit(_take)/gather | solution.py:31
  (86 shorter events, 40.3 us)
Async XLA Ops:
  7.2 6.0 %copy-start = (f32[16]{0:T(128)S(1)}, f32[16]{0:T(128)}, u32[]{:S(2)}) copy-start(f32[16]{0:T(128)} %param.17) | copy-start | bytes 196
  7.2 53.2 %reduce-scatter.2.cloned.1.call-start = ((), (), s32[]{:S(2)}) async-start(), calls=%async_computation.1 | async-start | bytes 147456 | tf_op jit(solution)/shard_map/reduce_scatter | solution.py:56
  9.0 17.0 %collective-permute-start.1 = (f32[256,128]{1,0:T(8,128)S(1)}, f32[256,128]{1,0:T(8,128)S(1)}, u32[]{:S(2)}, u32[]{:S(2)}) collective-permute-start(f32[256,128]{1,0:T(8,128)S(1)} %bitcast_select_fusion), channel_id=1, source_target_pairs={{1,0},{2,1},{3,2},{4,3},{5,4},{6,5},{7,6},{0,7},{9,8},{10,9},{11,1... | collective-permute-start | bytes 393224 | tf_op jit(solution)/shard_map/ppermute | solution.py:20
  12.4 13.6 %collective-permute-start = (f32[256,128]{1,0:T(8,128)S(1)}, f32[256,128]{1,0:T(8,128)S(1)}, u32[]{:S(2)}, u32[]{:S(2)}) collective-permute-start(f32[256,128]{1,0:T(8,128)S(1)} %bitcast_select_fusion), channel_id=1, source_target_pairs={{0,1},{1,2},{2,3},{3,4},{4,5},{5,6},{6,7},{7,0},{8,9},{9,10},{10,1... | collective-permute-start | bytes 393224 | tf_op jit(solution)/shard_map/ppermute | solution.py:18
  26.1 47.8 %copy-start.5 = (f32[16,256]{1,0:T(8,128)S(1)}, f32[16,256]{1,0:T(8,128)}, u32[]{:S(2)}) copy-start(f32[16,256]{1,0:T(8,128)} %param.15) | copy-start | bytes 49156
  74.5 16.8 %copy-start.6 = (f32[16,256]{1,0:T(8,128)S(1)}, f32[16,256]{1,0:T(8,128)}, u32[]{:S(2)}) copy-start(f32[16,256]{1,0:T(8,128)} %param.14) | copy-start | bytes 49156
  74.5 16.8 %copy-start.7 = (f32[16,256]{1,0:T(8,128)S(1)}, f32[16,256]{1,0:T(8,128)}, u32[]{:S(2)}) copy-start(f32[16,256]{1,0:T(8,128)} %param.13) | copy-start | bytes 49156
  78.1 14.5 %copy-start.8 = (s32[128]{0:T(128)S(1)}, s32[128]{0:T(128)}, u32[]{:S(2)}) copy-start(s32[128]{0:T(128)} %param.11) | copy-start | bytes 1540
  92.6 17.7 %copy-start.3 = (f32[256,128]{1,0:T(8,128)}, f32[256,128]{1,0:T(8,128)S(1)}, u32[]{:S(2)}) copy-start(f32[256,128]{1,0:T(8,128)S(1)} %add_reduce_fusion.7) | copy-start | bytes 393220
  92.7 3.0 %collective-permute-start.3 = (f32[256,128]{1,0:T(8,128)S(1)}, f32[256,128]{1,0:T(8,128)S(1)}, u32[]{:S(2)}, u32[]{:S(2)}) collective-permute-start(f32[256,128]{1,0:T(8,128)S(1)} %fusion.5), channel_id=1, source_target_pairs={{1,0},{2,1},{3,2},{4,3},{5,4},{6,5},{7,6},{0,7},{9,8},{10,9},{11,1... | collective-permute-start | bytes 393224 | tf_op jit(solution)/shard_map/ppermute | solution.py:20
  92.8 6.7 %collective-permute-start.2 = (f32[256,128]{1,0:T(8,128)S(1)}, f32[256,128]{1,0:T(8,128)S(1)}, u32[]{:S(2)}, u32[]{:S(2)}) collective-permute-start(f32[256,128]{1,0:T(8,128)S(1)} %fusion.5), channel_id=1, source_target_pairs={{0,1},{1,2},{2,3},{3,4},{4,5},{5,6},{6,7},{7,0},{8,9},{9,10},{10,1... | collective-permute-start | bytes 393224 | tf_op jit(solution)/shard_map/ppermute | solution.py:18
  113.2 3.8 %collective-permute-start.5 = (f32[256,128]{1,0:T(8,128)S(1)}, f32[256,128]{1,0:T(8,128)S(1)}, u32[]{:S(2)}, u32[]{:S(2)}) collective-permute-start(f32[256,128]{1,0:T(8,128)S(1)} %min.49), channel_id=1, source_target_pairs={{1,0},{2,1},{3,2},{4,3},{5,4},{6,5},{7,6},{0,7},{9,8},{10,9},{11,1... | collective-permute-start | bytes 393224 | tf_op jit(solution)/shard_map/ppermute | solution.py:20
  113.3 6.0 %collective-permute-start.4 = (f32[256,128]{1,0:T(8,128)S(1)}, f32[256,128]{1,0:T(8,128)S(1)}, u32[]{:S(2)}, u32[]{:S(2)}) collective-permute-start(f32[256,128]{1,0:T(8,128)S(1)} %min.49), channel_id=1, source_target_pairs={{0,1},{1,2},{2,3},{3,4},{4,5},{5,6},{6,7},{7,0},{8,9},{9,10},{10,1... | collective-permute-start | bytes 393224 | tf_op jit(solution)/shard_map/ppermute | solution.py:18
  133.0 3.8 %collective-permute-start.7 = (f32[256,128]{1,0:T(8,128)S(1)}, f32[256,128]{1,0:T(8,128)S(1)}, u32[]{:S(2)}, u32[]{:S(2)}) collective-permute-start(f32[256,128]{1,0:T(8,128)S(1)} %min.51), channel_id=1, source_target_pairs={{1,0},{2,1},{3,2},{4,3},{5,4},{6,5},{7,6},{0,7},{9,8},{10,9},{11,1... | collective-permute-start | bytes 393224 | tf_op jit(solution)/shard_map/ppermute | solution.py:20
  133.5 5.3 %collective-permute-start.6 = (f32[256,128]{1,0:T(8,128)S(1)}, f32[256,128]{1,0:T(8,128)S(1)}, u32[]{:S(2)}, u32[]{:S(2)}) collective-permute-start(f32[256,128]{1,0:T(8,128)S(1)} %min.51), channel_id=1, source_target_pairs={{0,1},{1,2},{2,3},{3,4},{4,5},{5,6},{6,7},{7,0},{8,9},{9,10},{10,1... | collective-permute-start | bytes 393224 | tf_op jit(solution)/shard_map/ppermute | solution.py:18
  152.5 3.8 %collective-permute-start.9 = (f32[256,128]{1,0:T(8,128)S(1)}, f32[256,128]{1,0:T(8,128)S(1)}, u32[]{:S(2)}, u32[]{:S(2)}) collective-permute-start(f32[256,128]{1,0:T(8,128)S(1)} %min.53), channel_id=1, source_target_pairs={{1,0},{2,1},{3,2},{4,3},{5,4},{6,5},{7,6},{0,7},{9,8},{10,9},{11,1... | collective-permute-start | bytes 393224 | tf_op jit(solution)/shard_map/ppermute | solution.py:20
  153.3 5.3 %collective-permute-start.8 = (f32[256,128]{1,0:T(8,128)S(1)}, f32[256,128]{1,0:T(8,128)S(1)}, u32[]{:S(2)}, u32[]{:S(2)}) collective-permute-start(f32[256,128]{1,0:T(8,128)S(1)} %min.53), channel_id=1, source_target_pairs={{0,1},{1,2},{2,3},{3,4},{4,5},{5,6},{6,7},{7,0},{8,9},{9,10},{10,1... | collective-permute-start | bytes 393224 | tf_op jit(solution)/shard_map/ppermute | solution.py:18
  172.3 3.8 %collective-permute-start.11 = (f32[256,128]{1,0:T(8,128)S(1)}, f32[256,128]{1,0:T(8,128)S(1)}, u32[]{:S(2)}, u32[]{:S(2)}) collective-permute-start(f32[256,128]{1,0:T(8,128)S(1)} %min.55), channel_id=1, source_target_pairs={{1,0},{2,1},{3,2},{4,3},{5,4},{6,5},{7,6},{0,7},{9,8},{10,9},{11,1... | collective-permute-start | bytes 393224 | tf_op jit(solution)/shard_map/ppermute | solution.py:20
  172.8 5.3 %collective-permute-start.10 = (f32[256,128]{1,0:T(8,128)S(1)}, f32[256,128]{1,0:T(8,128)S(1)}, u32[]{:S(2)}, u32[]{:S(2)}) collective-permute-start(f32[256,128]{1,0:T(8,128)S(1)} %min.55), channel_id=1, source_target_pairs={{0,1},{1,2},{2,3},{3,4},{4,5},{5,6},{6,7},{7,0},{8,9},{9,10},{10,1... | collective-permute-start | bytes 393224 | tf_op jit(solution)/shard_map/ppermute | solution.py:18
  191.8 6.2 %copy-start.1 = (f32[256,128]{1,0:T(8,128)}, f32[256,128]{1,0:T(8,128)S(1)}, u32[]{:S(2)}) copy-start(f32[256,128]{1,0:T(8,128)S(1)} %add_reduce_fusion.2) | copy-start | bytes 393220
  191.8 3.8 %collective-permute-start.13 = (f32[256,128]{1,0:T(8,128)S(1)}, f32[256,128]{1,0:T(8,128)S(1)}, u32[]{:S(2)}, u32[]{:S(2)}) collective-permute-start(f32[256,128]{1,0:T(8,128)S(1)} %min.57), channel_id=1, source_target_pairs={{1,0},{2,1},{3,2},{4,3},{5,4},{6,5},{7,6},{0,7},{9,8},{10,9},{11,1... | collective-permute-start | bytes 393224 | tf_op jit(solution)/shard_map/ppermute | solution.py:20
  192.7 5.3 %collective-permute-start.12 = (f32[256,128]{1,0:T(8,128)S(1)}, f32[256,128]{1,0:T(8,128)S(1)}, u32[]{:S(2)}, u32[]{:S(2)}) collective-permute-start(f32[256,128]{1,0:T(8,128)S(1)} %min.57), channel_id=1, source_target_pairs={{0,1},{1,2},{2,3},{3,4},{4,5},{5,6},{6,7},{7,0},{8,9},{9,10},{10,1... | collective-permute-start | bytes 393224 | tf_op jit(solution)/shard_map/ppermute | solution.py:18
  211.6 3.8 %collective-permute-start.15 = (f32[256,128]{1,0:T(8,128)S(1)}, f32[256,128]{1,0:T(8,128)S(1)}, u32[]{:S(2)}, u32[]{:S(2)}) collective-permute-start(f32[256,128]{1,0:T(8,128)S(1)} %min.59), channel_id=1, source_target_pairs={{1,0},{2,1},{3,2},{4,3},{5,4},{6,5},{7,6},{0,7},{9,8},{10,9},{11,1... | collective-permute-start | bytes 393224 | tf_op jit(solution)/shard_map/ppermute | solution.py:20
  212.2 5.3 %collective-permute-start.14 = (f32[256,128]{1,0:T(8,128)S(1)}, f32[256,128]{1,0:T(8,128)S(1)}, u32[]{:S(2)}, u32[]{:S(2)}) collective-permute-start(f32[256,128]{1,0:T(8,128)S(1)} %min.59), channel_id=1, source_target_pairs={{0,1},{1,2},{2,3},{3,4},{4,5},{5,6},{6,7},{7,0},{8,9},{9,10},{10,1... | collective-permute-start | bytes 393224 | tf_op jit(solution)/shard_map/ppermute | solution.py:18
  (2 other events, 1.9 us)
Sparse Core Ops, SparseCore 0:
  25.3 35.0 reduce-scatter.1
